TPU v7x, 32 devices: a whole 2x2x4 slice. The times are simulated.
32 devices in a mesh: dp: 4 (over x, y), ep: 8 (over z, core).
Axes of the slice: x: 2, y: 2, z: 4, core: 2. Of those that a mesh axis runs over, the one named last changes fastest.
Arguments:
- x: bfloat16 [4, 8, 256, 5120], P('dp', 'ep'), parts along dimension 0
- expert: int32 [4, 8, 256, 6], P('dp', 'ep'), parts along dimension 0
- slot: int32 [4, 8, 256, 6], P('dp', 'ep'), parts along dimension 0
- gate: float32 [4, 8, 256, 6], P('dp', 'ep'), parts along dimension 0
- w_gate: bfloat16 [40, 5120, 1536], P('ep')
- w_up: bfloat16 [40, 5120, 1536], P('ep')
- w_down: bfloat16 [40, 1536, 5120], P('ep')
- s_gate: bfloat16 [5120, 3072], replicated
- s_up: bfloat16 [5120, 3072], replicated
- s_down: bfloat16 [3072, 5120], replicated
Outputs:
- y: bfloat16 [4, 8, 256, 5120], P('dp', 'ep'), parts along dimension 0
There are 4 independent parts. A program takes and returns all parts, laid end to end along the dimension named above; an argument that names none is the same for every part.
All inputs are finite; a program needn't handle non-finite values.
Results may differ from a plain program's by a relative error of at most 0.009.
Values are sent between devices in bfloat16 or wider.
A program may use at most 2 GiB of HBM per device.

v0:
```python
import jax
import jax.numpy as jnp
from jax import lax
from jax.sharding import NamedSharding, PartitionSpec as P


def einsum(form, a, b):
    return jnp.einsum(form, a.astype(jnp.float32), b.astype(jnp.float32))


def for_all(x, s_gate, s_up, s_down):
    h = jax.nn.silu(einsum("...d,df->...f", x, s_gate)) * einsum("...d,df->...f", x, s_up)
    return einsum("...f,fd->...d", h.astype(jnp.bfloat16), s_down)


def solution(mesh):
    def placed(v, *spec):
        return lax.with_sharding_constraint(v, NamedSharding(mesh, P(*spec)))

    def step(x, expert, slot, gate, w_gate, w_up, w_down, s_gate, s_up, s_down):
        experts, (tokens, top) = w_gate.shape[0], expert.shape[2:]
        slots = 5 * tokens * top // (4 * experts)
        to_expert = jax.nn.one_hot(expert, experts, dtype=jnp.bfloat16)
        to_slot = jax.nn.one_hot(slot, slots, dtype=jnp.bfloat16)
        weighted = to_expert * gate[..., None].astype(jnp.bfloat16)
        dispatch = einsum("abtke,abtkc->abtec", to_expert, to_slot).astype(jnp.bfloat16)
        combine = einsum("abtke,abtkc->abtec", weighted, to_slot).astype(jnp.bfloat16)
        z = einsum("abtec,abtd->aebcd", dispatch, x).astype(jnp.bfloat16)
        z = placed(z, "dp", None, "ep", None, None)
        z = placed(z, "dp", "ep", None, None, None)
        h = jax.nn.silu(einsum("aebcd,edf->aebcf", z, w_gate))
        h = (h * einsum("aebcd,edf->aebcf", z, w_up)).astype(jnp.bfloat16)
        out = einsum("aebcf,efd->aebcd", h, w_down).astype(jnp.bfloat16)
        out = placed(out, "dp", "ep", None, None, None)
        out = placed(out, "dp", None, "ep", None, None)
        y = einsum("abtec,aebcd->abtd", combine, out)
        return (y + for_all(x, s_gate, s_up, s_down)).astype(jnp.bfloat16)

    return step
```

profile of v0, /device:TPU:1, one launch (start us, length us, event | category | flops | bytes accessed | tf_op | source)
XLA Modules:
  0.0 1055.4 jit_solution(16032586320603323284)
XLA Ops:
  0.0 0.0 copy-start
  0.0 1.0 copy.21
  1.0 0.0 copy-start.1
  1.0 0.8 copy.23
  1.8 0.0 copy-start.3
  1.9 2.9 convolution_convert_fusion.1
  4.8 0.0 copy-done
  4.8 9.6 convolution_convert_fusion
  14.4 0.0 copy-done.1
  14.4 0.0 copy-done.3
  14.4 434.2 %all-to-all.4 = bf16[1,8,5,1,48,5120]{5,4,2,3,0,1:T(8,128)(2,1)} all-to-all(bf16[1,8,5,1,48,5120]{5,4,2,3,0,1:T(8,128)(2,1)} %bitcast.111), channel_id=1, replica_groups=mesh['dp'=4,'ep'=8] {'ep'}, dimensions={1} | all-to-all | bytes 39321600 | tf_op jit(solution)/sharding_constraint;jit(solution)/sharding_constraint | solution.py:18
  448.6 43.5 %fusion.4 = f32[5,8,48,1536]{3,2,1,0:T(8,128)} fusion(bf16[5,5120,1536]{2,1,0:T(8,128)(2,1)} %param.4, bf16[1,8,5,1,48,5120]{5,4,2,3,0,1:T(8,128)(2,1)} %all-to-all.4), kind=kOutput, calls=%fused_computation.4 | convolution fusion | flops 30198988800 | bytes 110100480 | tf_op jit(solution)/aebcd,edf->aebcf/dot_general | solution.py:8
  492.0 43.6 %fusion.12 = bf16[1,5,8,48,1536]{4,3,2,1,0:T(8,128)(2,1)} fusion(f32[5,8,48,1536]{3,2,1,0:T(8,128)} %fusion.4, bf16[5,5120,1536]{2,1,0:T(8,128)(2,1)} %param.5, bf16[1,8,5,1,48,5120]{5,4,2,3,0,1:T(8,128)(2,1)} %all-to-all.4), kind=kOutput, calls=%fused_computation.13 | convolution fusion | flops 30216683520 | bytes 115998720 | tf_op jit(solution)/aebcd,edf->aebcf/dot_general | solution.py:8
  535.7 45.9 %convert_bitcast_fusion = bf16[1,5,8,1,48,5120]{5,4,2,1,3,0:T(8,128)(2,1)} fusion(bf16[5,1536,5120]{2,1,0:T(8,128)(2,1)} %param.6, bf16[1,5,8,48,1536]{4,3,2,1,0:T(8,128)(2,1)} %fusion.12), kind=kOutput, calls=%fused_computation.8 | convolution fusion | flops 30208819200 | bytes 104202240 | tf_op jit(solution)/aebcf,efd->aebcd/dot_general | solution.py:8
  581.5 16.3 %copy.15 = bf16[1,5,8,1,48,5120]{5,4,1,3,0,2:T(8,128)(2,1)} copy(bf16[1,5,8,1,48,5120]{5,4,2,1,3,0:T(8,128)(2,1)} %convert_bitcast_fusion) | data formatting | bytes 39321600 | tf_op jit(solution)/sharding_constraint;jit(solution)/sharding_constraint | solution.py:18
  597.9 0.0 copy-start.5
  597.9 0.0 copy-start.2
  597.9 0.0 copy-start.4
  597.9 20.5 %all-to-all-start.1 = ((bf16[1,5,8,1,48,5120]{5,4,1,3,0,2:T(8,128)(2,1)}), bf16[1,5,8,1,48,5120]{5,4,1,3,0,2:T(8,128)(2,1)}, u32[]{:S(2)}, u32[]{:S(2)}) async-start(bf16[1,5,8,1,48,5120]{5,4,1,3,0,2:T(8,128)(2,1)} %copy.15), calls=%async_computation.1 | async-start | bytes 39321600 | tf_op jit(solution)/sharding_constraint;jit(solution)/sharding_constraint | solution.py:18
  618.4 0.0 copy-done.5
  618.4 0.1 copy.22
  618.5 0.0 copy-done.2
  618.5 0.0 copy-done.4
  618.5 4.2 convolution_convert_fusion.2
  622.8 16.0 %convolution_bitcast_fusion.2 = f32[1,1,256,3072]{3,2,1,0:T(8,128)} fusion(bf16[5120,3072]{1,0:T(8,128)(2,1)} %param.7, bf16[1,1,256,5120]{3,2,1,0:T(8,128)(2,1)S(1)} %copy-done), kind=kOutput, calls=%fused_computation.26 | convolution fusion | flops 8053063680 | bytes 37224448 | tf_op jit(solution)/...d,df->...f/dot_general | solution.py:8
  638.8 30.1 %fusion.27 = f32[256,5120]{1,0:T(8,128)} fusion(bf16[3072,5120]{1,0:T(8,128)(2,1)} %param.9, bf16[5120,3072]{1,0:T(8,128)(2,1)} %param.8, f32[1,1,256,3072]{3,2,1,0:T(8,128)} %convolution_bitcast_fusion.2, bf16[1,1,256,5120]{3,2,1,0:T(8,128)(2,1)S(1)} %copy-done), kind=kOutput, calls=%fused_computation.29 | convolution fusion | flops 16110845952 | bytes 73924608 | tf_op jit(solution)/...f,fd->...d/dot_general | solution.py:8
  668.9 373.4 %all-to-all-done.1 = bf16[1,5,8,1,48,5120]{5,4,1,3,0,2:T(8,128)(2,1)} async-done(((bf16[1,5,8,1,48,5120]{5,4,1,3,0,2:T(8,128)(2,1)}), bf16[1,5,8,1,48,5120]{5,4,1,3,0,2:T(8,128)(2,1)}, u32[]{:S(2)}, u32[]{:S(2)}) %all-to-all-start.1) | async-done | bytes 19660832 | tf_op jit(solution)/sharding_constraint;jit(solution)/sharding_constraint | solution.py:18
  1042.2 13.2 %fusion.18 = bf16[1,1,256,5120]{3,2,1,0:T(8,128)(2,1)} fusion(f32[256,5120]{1,0:T(8,128)} %fusion.27, bf16[40,48,5120]{2,1,0:T(8,128)(2,1)} %bitcast.25, bf16[256,40,48]{2,1,0:T(8,128)(2,1)} %convolution_convert_fusion.2), kind=kOutput, calls=%fused_computation.22 | convolution fusion | flops 5035786240 | bytes 28508160 | tf_op jit(solution)/abtec,aebcd->abtd/dot_general | solution.py:8
  (1 shorter events, 0.0 us)
Async XLA Ops:
  0.0 4.8 copy-start
  1.0 13.4 %copy-start.1 = (s32[1,1,256,6]{3,2,1,0:T(8,128)}, s32[1,1,256,6]{3,2,1,0:T(8,128)S(1)}, u32[]{:S(2)}) copy-start(s32[1,1,256,6]{3,2,1,0:T(8,128)S(1)} %copy.21) | copy-start | bytes 18436
  1.8 12.5 %copy-start.3 = (s32[1,1,256,6]{3,2,1,0:T(8,128)}, s32[1,1,256,6]{3,2,1,0:T(8,128)S(1)}, u32[]{:S(2)}) copy-start(s32[1,1,256,6]{3,2,1,0:T(8,128)S(1)} %copy.23) | copy-start | bytes 18436
  597.9 20.5 %copy-start.5 = (f32[1,1,256,6]{2,1,3,0:T(1,128)S(1)}, f32[1,1,256,6]{2,1,3,0:T(1,128)}, u32[]{:S(2)}) copy-start(f32[1,1,256,6]{2,1,3,0:T(1,128)} %param.1) | copy-start | bytes 18436
  597.9 20.7 %copy-start.2 = (s32[1,1,256,6]{3,2,1,0:T(8,128)S(1)}, s32[1,1,256,6]{3,2,1,0:T(8,128)}, u32[]{:S(2)}) copy-start(s32[1,1,256,6]{3,2,1,0:T(8,128)} %copy-done.1) | copy-start | bytes 18436
  597.9 20.7 %copy-start.4 = (s32[1,1,256,6]{3,2,1,0:T(8,128)S(1)}, s32[1,1,256,6]{3,2,1,0:T(8,128)}, u32[]{:S(2)}) copy-start(s32[1,1,256,6]{3,2,1,0:T(8,128)} %copy-done.3) | copy-start | bytes 18436
  597.9 444.4 %all-to-all-start.1 = ((bf16[1,5,8,1,48,5120]{5,4,1,3,0,2:T(8,128)(2,1)}), bf16[1,5,8,1,48,5120]{5,4,1,3,0,2:T(8,128)(2,1)}, u32[]{:S(2)}, u32[]{:S(2)}) async-start(bf16[1,5,8,1,48,5120]{5,4,1,3,0,2:T(8,128)(2,1)} %copy.15), calls=%async_computation.1 | async-start | bytes 39321600 | tf_op jit(solution)/sharding_constraint;jit(solution)/sharding_constraint | solution.py:18
where the time goes:
time: 1060 us
  blocking collectives  434 us (41%)
  waiting for transfers between devices  373 us (35%)
  matrix products  209 us (20%)
  starting transfers between devices  20.5 us (2%)
  local copies, waits for them, and re-layouts  18.3 us (2%)
    another operation x1, blocking collectives, placed(): return lax.with_sharding_constraint(v, NamedSharding(mesh, P(*spec)))  434 us
    another operation x1, waiting for transfers between devices, placed(): return lax.with_sharding_constraint(v, NamedSharding(mesh, P(*spec)))  373 us
    dot_general x9, matrix products, einsum(): return jnp.einsum(form, a.astype(jnp.float32), b.astype(jnp.float32))  209 us
  transfers between devices with their start and end apart: 1, of which 1 were waited for; matrix products, arithmetic and copies ran while one was open for 5% of the time, Pallas kernels for 0%

commit v1 on v0

v1 whole, which is shorter than its diff:
```python
import jax
import jax.numpy as jnp
from jax import lax
from jax.sharding import PartitionSpec as P

F32 = jnp.float32
BF16 = jnp.bfloat16


def dot(form, a, b):
    return jnp.einsum(form, a, b, preferred_element_type=F32)


def solution(mesh):
    members = mesh.shape["ep"]

    def local(x, expert, slot, gate, w_gate, w_up, w_down, s_gate, s_up, s_down):
        own, (tokens, top) = w_gate.shape[0], expert.shape[2:]
        experts = own * members
        slots = 5 * tokens * top // (4 * experts)
        rows = own * slots
        x = x[0, 0]
        me = lax.axis_index("ep")
        place = jnp.where(slot[0, 0] < slots, expert[0, 0] * slots + slot[0, 0], -1)
        place = lax.all_gather(place, "ep") - me * rows
        gates = lax.all_gather(gate[0, 0], "ep").astype(BF16)
        hit = place[..., None] == lax.broadcasted_iota(jnp.int32, (1, 1, 1, rows), 3)
        dispatch = jnp.any(hit, axis=2).astype(BF16)
        combine = jnp.sum(jnp.where(hit, gates[..., None].astype(F32), 0.0), axis=2).astype(BF16)

        everyone = lax.all_gather(x, "ep")
        a = jax.nn.silu(dot("td,df->tf", x, s_gate)) * dot("td,df->tf", x, s_up)
        shared = dot("tf,fd->td", a.astype(BF16), s_down)
        z = dot("btr,btd->brd", dispatch, everyone).astype(BF16)
        z = z.reshape(members, own, slots, -1)
        h = jax.nn.silu(dot("becd,edf->ebcf", z, w_gate)) * dot("becd,edf->ebcf", z, w_up)
        out = dot("ebcf,efd->becd", h.astype(BF16), w_down).astype(BF16)
        out = out.reshape(members, rows, -1)
        y = dot("btr,brd->btd", combine, out).astype(BF16)
        y = lax.psum_scatter(y, "ep", scatter_dimension=0, tiled=False)
        return (y.astype(F32) + shared).astype(BF16)[None, None]

    by_token = P("dp", "ep", None, None)
    by_expert = P("ep", None, None)
    whole = P(None, None)
    return jax.shard_map(
        local,
        mesh=mesh,
        in_specs=(by_token,) * 4 + (by_expert,) * 3 + (whole,) * 3,
        out_specs=by_token,
        check_vma=False,
    )
```

time: 1060 us -> 633 us (0.60)
  blocking collectives: 434 us -> 33.5 us
  waiting for transfers between devices: 373 us -> 336 us
  starting transfers between devices: 20.5 us -> 0.04 us
  between operations: 0.07 us -> 13.4 us
  matrix products: 209 us -> 220 us
    another operation x1 -> x0, blocking collectives: 434 us -> none  [placed(): return lax.with_sharding_constraint(v, NamedSharding(mesh, P(*spec)))]
    another operation x1 -> x0, waiting for transfers between devices: 373 us -> none  [placed(): return lax.with_sharding_constraint(v, NamedSharding(mesh, P(*spec)))]
    reduce_scatter x0 -> x1, waiting for transfers between devices: none -> 186 us  [local(): y = lax.psum_scatter(y, 'ep', scatter_dimension=0, tiled=False)]
    all_gather x0 -> x1, waiting for transfers between devices: none -> 149 us  [local(): everyone = lax.all_gather(x, 'ep')]
    all_gather x0 -> x2, blocking collectives: none -> 33.5 us  [the longest x1 18 us: local(): gates = lax.all_gather(gate[0, 0], 'ep').astype(BF16)]
    another operation x1 -> x0, starting transfers between devices: 20.5 us -> none  [placed(): return lax.with_sharding_constraint(v, NamedSharding(mesh, P(*spec)))]
    convert_element_type x1 -> x2, local copies, waits for them, and re-layouts: 0.15 us -> 16.6 us  [the longest x1 16.5 us: local(): out = dot('ebcf,efd->becd', h.astype(BF16), w_down).astype(BF16)]
    another operation x1 -> x0, local copies, waits for them, and re-layouts: 16.3 us -> none  [placed(): return lax.with_sharding_constraint(v, NamedSharding(mesh, P(*spec)))]
  transfers between devices with their start and end apart: 1 -> 2, of which waited for: 1 -> 2; matrix products, arithmetic and copies ran while one was open for 5% -> 4% of each run, Pallas kernels for 0% -> 0%
where the time goes in v1:
time: 633 us; the launch traced here: 630 us
  waiting for transfers between devices  336 us (53%)
  matrix products  220 us (35%)
  blocking collectives  33.5 us (5%)
  local copies, waits for them, and re-layouts  18.3 us (3%)
  between operations  13.4 us (2%)
  other arithmetic  7.71 us (1%)
    dot_general x7, matrix products, dot(): return jnp.einsum(form, a, b, preferred_element_type=F32)  220 us
    reduce_scatter x1, waiting for transfers between devices, local(): y = lax.psum_scatter(y, 'ep', scatter_dimension=0, tiled=False)  186 us
    all_gather x1, waiting for transfers between devices, local(): everyone = lax.all_gather(x, 'ep')  149 us
    all_gather x1, blocking collectives, local(): gates = lax.all_gather(gate[0, 0], 'ep').astype(BF16)  18 us
    convert_element_type x1, local copies, waits for them, and re-layouts, local(): out = dot('ebcf,efd->becd', h.astype(BF16), w_down).astype(BF16)  16.5 us
    all_gather x1, blocking collectives, local(): place = lax.all_gather(place, 'ep') - me * rows  15.5 us
  transfers between devices with their start and end apart: 2, of which 2 were waited for; matrix products, arithmetic and copies ran while one was open for 4% of the time, Pallas kernels for 0%

profile of v1, /device:TPU:1, one launch (start us, length us, event | category | flops | bytes accessed | tf_op | source)
XLA Modules:
  0.0 629.6 jit_solution(11656026776172361999)
XLA Ops:
  6.5 0.0 all-gather.5.cloned.1.call-start
  6.5 0.7 all-gather.5.cloned.1.call-update
  7.3 0.0 reduce-scatter.2.cloned.1.call-start
  7.3 0.7 compare_select_fusion
  8.0 15.5 %all-gather = s32[8,1,256,6]{2,1,3,0:T(1,128)S(1)} all-gather(s32[1,1,256,6]{2,1,3,0:T(1,128)S(1)} %compare_select_fusion), channel_id=2, replica_groups=mesh['dp'=4,'ep'=8] {'ep'}, dimensions={0}, use_global_device_ids=true | all-gather | bytes 55296 | tf_op jit(solution)/shard_map/all_gather | solution.py:25
  23.5 0.7 convert.5
  24.2 18.0 %all-gather.1 = bf16[8,1,256,6]{2,1,3,0:T(2,128)(2,1)S(1)} all-gather(bf16[1,1,256,6]{2,1,3,0:T(2,128)(2,1)S(1)} %convert.5), channel_id=3, replica_groups=mesh['dp'=4,'ep'=8] {'ep'}, dimensions={0}, use_global_device_ids=true | all-gather | bytes 27648 | tf_op jit(solution)/shard_map/all_gather | solution.py:26
  42.3 3.2 fusion.15
  45.5 3.1 select_reduce_fusion
  48.6 149.4 %all-gather.5.cloned.1.call-done = bf16[8,1,256,5120]{3,2,1,0:T(8,128)(2,1)} async-done(((bf16[1,1,256,5120]{3,2,1,0:T(8,128)(2,1)}), bf16[8,1,256,5120]{3,2,1,0:T(8,128)(2,1)}) %all-gather.5.cloned.1.call-update) | async-done | bytes 20971536 | tf_op jit(solution)/shard_map/all_gather | solution.py:31
  198.0 20.8 %fusion.12 = bf16[8,240,5120]{2,1,0:T(8,128)(2,1)} fusion(pred[8,256,240]{1,2,0:T(8,128)(4,1)S(1)} %fusion.15, bf16[8,1,256,5120]{3,2,1,0:T(8,128)(2,1)} %all-gather.5.cloned.1.call-done), kind=kOutput, calls=%fused_computation.12 | convolution fusion | flops 5042995200 | bytes 41123840 | tf_op jit(solution)/shard_map/btr,btd->brd/dot_general | solution.py:11
  218.8 44.0 %fusion.2 = f32[5,8,48,1536]{3,2,1,0:T(8,128)} fusion(bf16[5,5120,1536]{2,1,0:T(8,128)(2,1)} %param.15, bf16[8,5,48,5120]{3,2,1,0:T(8,128)(2,1)} %bitcast.53), kind=kOutput, calls=%fused_computation.2 | convolution fusion | flops 30198988800 | bytes 110100480 | tf_op jit(solution)/shard_map/becd,edf->ebcf/dot_general | solution.py:11
  262.7 43.4 %fusion.4 = f32[5,8,48,1536]{3,2,1,0:T(8,128)} fusion(bf16[5,5120,1536]{2,1,0:T(8,128)(2,1)} %param.14, bf16[8,5,48,5120]{3,2,1,0:T(8,128)(2,1)} %bitcast.54), kind=kOutput, calls=%fused_computation.4 | convolution fusion | flops 30198988800 | bytes 110100480 | tf_op jit(solution)/shard_map/becd,edf->ebcf/dot_general | solution.py:11
  306.2 47.2 %convert_bitcast_fusion = bf16[8,5,48,5120]{3,2,0,1:T(8,128)(2,1)} fusion(bf16[5,1536,5120]{2,1,0:T(8,128)(2,1)} %param.16, f32[5,8,48,1536]{3,2,1,0:T(8,128)} %fusion.2, f32[5,8,48,1536]{3,2,1,0:T(8,128)} %fusion.4), kind=kOutput, calls=%fused_computation.8 | convolution fusion | flops 30226513920 | bytes 121896960 | tf_op jit(solution)/shard_map/ebcf,efd->becd/dot_general | solution.py:11
  353.4 0.0 copy-start
  353.4 16.5 %copy.39 = bf16[8,5,48,5120]{3,2,1,0:T(8,128)(2,1)} copy(bf16[8,5,48,5120]{3,2,0,1:T(8,128)(2,1)} %convert_bitcast_fusion) | data formatting | bytes 39321600 | tf_op jit(solution)/shard_map/convert_element_type | solution.py:37
  369.9 0.0 copy-done
  369.9 18.3 %convolution_convert_fusion = bf16[8,256,5120]{2,1,0:T(8,128)(2,1)} fusion(bf16[8,240,5120]{2,1,0:T(8,128)(2,1)} %bitcast.52, bf16[8,256,240]{1,2,0:T(8,128)(2,1)S(1)} %copy-done), kind=kOutput, calls=%fused_computation.11 | convolution fusion | flops 5043650560 | bytes 41615360 | tf_op jit(solution)/shard_map/btr,brd->btd/dot_general | solution.py:11
  388.3 0.0 copy-start.1
  388.3 0.0 reduce-scatter.2.cloned.1.call-update
  388.3 1.7 copy-done.1
  390.0 15.9 %fusion.27 = f32[256,3072]{1,0:T(8,128)} fusion(bf16[5120,3072]{1,0:T(8,128)(2,1)} %param.17, bf16[1,1,256,5120]{3,2,1,0:T(8,128)(2,1)S(1)} %copy-done.1), kind=kOutput, calls=%fused_computation.29 | convolution fusion | flops 8053063680 | bytes 37224448 | tf_op jit(solution)/shard_map/td,df->tf/dot_general | solution.py:11
  405.9 186.2 %reduce-scatter.2.cloned.1.call-done = bf16[1,256,5120]{2,1,0:T(8,128)(2,1)} async-done(((bf16[8,256,5120]{2,1,0:T(8,128)(2,1)}), bf16[1,256,5120]{2,1,0:T(8,128)(2,1)}) %reduce-scatter.2.cloned.1.call-update) | async-done | bytes 2621456 | tf_op jit(solution)/shard_map/reduce_scatter | solution.py:40
  592.0 30.7 %fusion.17 = bf16[1,1,256,5120]{3,2,1,0:T(8,128)(2,1)} fusion(bf16[3072,5120]{1,0:T(8,128)(2,1)} %param.19, bf16[5120,3072]{1,0:T(8,128)(2,1)} %param.18, f32[256,3072]{1,0:T(8,128)} %fusion.27, bf16[1,256,5120]{2,1,0:T(8,128)(2,1)} %reduce-scatter.2.cloned.1.call-done, bf16[1,1,256,5120]{3,2,1,0:T(8,128)(2,1)S(1)} %copy-done.1), kind=kOutput, calls=%fused_computation.19 | convolution fusion | flops 16114778112 | bytes 73924608 | tf_op jit(solution)/shard_map/tf,fd->td/dot_general | solution.py:11
  (4 shorter events, 0.0 us)
Async XLA Ops:
  6.5 191.4 %all-gather.5.cloned.1.call-start = ((), (), s32[]{:S(2)}) async-start(), calls=%async_computation.2 | async-start | bytes 23592960 | tf_op jit(solution)/shard_map/all_gather | solution.py:31
  7.3 584.8 %reduce-scatter.2.cloned.1.call-start = ((), (), s32[]{:S(2)}) async-start(), calls=%async_computation.1 | async-start | bytes 23592960 | tf_op jit(solution)/shard_map/reduce_scatter | solution.py:40
  353.4 16.5 %copy-start = (bf16[8,256,240]{1,2,0:T(8,128)(2,1)S(1)}, bf16[8,256,240]{1,2,0:T(8,128)(2,1)}, u32[]{:S(2)}) copy-start(bf16[8,256,240]{1,2,0:T(8,128)(2,1)} %select_reduce_fusion) | copy-start | bytes 2949124
  388.3 1.7 copy-start.1
Sparse Core Ops, SparseCore 0:
  9.0 188.9 all-gather.4
  388.4 203.6 reduce-scatter.1

commit v2 on v1

v2 whole, which is shorter than its diff:
```python
import functools

import jax
import jax.numpy as jnp
from jax import lax
from jax.experimental import pallas as pl
from jax.experimental.pallas import tpu as pltpu
from jax.sharding import PartitionSpec as P

F32 = jnp.float32
BF16 = jnp.bfloat16
W = 256
NL = 6
NT = 6
MESH = pl.DeviceIdType.MESH


def mm(a, b):
    return jnp.dot(a, b, preferred_element_type=F32)


def kernel(
    x, disp, comb, wg, wu, wd, sg, su, sd, y,
    xg, acc, tot, h, sh, gring, dring, zb, ob, pb, dl, rl, ll, csr, csl, yb,
    agr, ags, gsem, dsem, dlr, dls, rrec, lrec, rsend, lsend, ysem, free_r, free_l, free_p,
):
    tokens, depth = x.shape
    own, _, ff = wg.shape
    slots = disp.shape[1] // own
    nq = depth // W
    deep = 2 * W
    me = lax.axis_index("ep")
    z, c = me // 2, me % 2
    left, right, partner = {"ep": me - 2}, {"ep": me + 2}, {"ep": z * 2 + 1 - c}

    def send(src, dst, ssem, rsem, to):
        return pltpu.make_async_remote_copy(
            src_ref=src, dst_ref=dst, send_sem=ssem, recv_sem=rsem, device_id=to, device_id_type=MESH
        )

    def signal(sem, to):
        pl.semaphore_signal(sem, inc=1, device_id=to, device_id_type=MESH)

    shared_tiles = 4 * (depth // deep)
    per_pass = 2 * own * (depth // deep)
    all_tiles = shared_tiles + 2 * per_pass

    def g_copy(src, slot):
        return pltpu.make_async_copy(src, gring.at[slot], gsem.at[slot])

    def g_start(g):
        slot = g % 4

        @pl.when(g < shared_tiles)
        def _():
            rows = pl.ds((g // 4) * deep, deep)
            t = g % 4

            @pl.when(t < 2)
            def _():
                g_copy(sg.at[rows, pl.ds(pl.multiple_of((t % 2) * ff, 128), ff)], slot).start()

            @pl.when(t >= 2)
            def _():
                g_copy(su.at[rows, pl.ds(pl.multiple_of((t % 2) * ff, 128), ff)], slot).start()

        @pl.when((g >= shared_tiles) & (g < all_tiles))
        def _():
            r = (g - shared_tiles) % per_pass
            rows = pl.ds((r // (2 * own)) * deep, deep)
            t = r % (2 * own)

            @pl.when(t < own)
            def _():
                g_copy(wg.at[t % own, rows, :], slot).start()

            @pl.when(t >= own)
            def _():
                g_copy(wu.at[t % own, rows, :], slot).start()

    def g_wait(g):
        g_copy(wg.at[0, pl.ds(0, deep), :], g % 4).wait()

    def d_copy(src, slot):
        return pltpu.make_async_copy(src, dring.at[slot], dsem.at[slot])

    def d_start(g, nt):
        slot = g % 4
        t = g % nt
        cols = pl.ds(pl.multiple_of((g // nt) * W, W), W)

        @pl.when((g < nq * nt) & (t < own))
        def _():
            d_copy(wd.at[t % own, :, cols], slot).start()

        @pl.when((g < nq * nt) & (t >= own))
        def _():
            d_copy(sd.at[pl.ds(((t - own) % 2) * ff, ff), cols], slot).start()

    def d_wait(g):
        d_copy(wd.at[0, :, pl.ds(0, W)], g % 4).wait()

    def hop(q, src, kind, to):
        piece = xg.at[c * nq + q, src]
        return send(piece, piece, ags.at[kind, src, q % 2], agr.at[c * nq + q, src], to)

    def hop_start(q, src, kind, to):
        @pl.when(q >= 2)
        def _():
            hop(q - 2, src, kind, to).wait_send()

        hop(q, src, kind, to).start()

    def spread(clock):
        for src in range(4):
            q = clock - c * nq - jnp.abs(z - src)

            @pl.when((q >= 0) & (q < nq))
            def _():
                @pl.when(z != src)
                def _():
                    hop(q, src, 0, right).wait_recv()

                @pl.when((z >= src) & (z < 3))
                def _():
                    hop_start(q, src, 0, right)

                @pl.when((z <= src) & (z > 0))
                def _():
                    hop_start(q, src, 1, left)

                hop_start(q, src, 2, partner)

    def own_piece(q):
        return pltpu.make_async_copy(
            x.at[:, pl.ds(pl.multiple_of(q * W, W), W)], xg.at[c * nq + q, z], agr.at[c * nq + q, z]
        )

    barrier = pltpu.get_barrier_semaphore()

    @pl.when(z > 0)
    def _():
        signal(barrier, left)

    @pl.when(z < 3)
    def _():
        signal(barrier, right)

    signal(barrier, partner)

    @pl.loop(0, nq)
    def _(q):
        own_piece(q).start()

    for g in range(3):
        g_start(jnp.int32(g))

    @pl.loop(0, 4 * NT)
    def _(b):
        tot[b] = jnp.zeros((tokens, W), F32)

    @pl.loop(0, 2 * own)
    def _(b):
        acc[b] = jnp.zeros((4 * slots, ff), F32)

    @pl.loop(0, nq)
    def _(q):
        own_piece(q).wait()

    pl.semaphore_wait(barrier, 1 + (z > 0).astype(jnp.int32) + (z < 3).astype(jnp.int32))

    @pl.loop(0, depth // deep)
    def _(k):
        @pl.when(k % 2 == 0)
        def _():
            spread(k // 2)

        @pl.loop(0, 4)
        def _(t):
            g = 4 * k + t
            g_start(g + 3)
            g_wait(g)
            a = [xg[c * nq + 2 * k + i, z] for i in range(2)]
            for n in range(ff // W):
                w = gring.at[g % 4, :, pl.ds(n * W, W)]
                tot[t * (ff // W) + n] += mm(a[0], w[:W]) + mm(a[1], w[W:])

    half = 2 * ff // W
    for n in range(half):
        v = tot[n]
        sh[n // (ff // W), :, pl.ds(n % (ff // W) * W, W)] = (jax.nn.silu(v) * tot[half + n]).astype(BF16)

    def up(u):
        s, k, part = u // nq, (u % nq) // 2, u % 2

        @pl.when(part == 0)
        def _():
            @pl.when(c != s)
            def _():
                for i in range(2):
                    for src in range(4):
                        piece = xg.at[s * nq + 2 * k + i, src]
                        send(piece, piece, ags.at[0, src, 0], agr.at[s * nq + 2 * k + i, src], partner).wait_recv()

            @pl.loop(0, 4)
            def _(src):
                for i in range(2):
                    v = mm(disp[2 * src + s], xg[s * nq + 2 * k + i, src]).astype(BF16)
                    for e in range(own):
                        zb[e, src, :, pl.ds(i * W, W)] = v[e * slots : (e + 1) * slots]

        @pl.loop(0, own)
        def _(e):
            g = shared_tiles + u * own + e
            g_start(g + 3)
            g_wait(g)
            a = zb[e].reshape(4 * slots, deep)
            for n in range(ff // 512):
                cols = pl.ds(n * 512, 512)
                acc[part * own + e, :, cols] += mm(a, gring[g % 4, :, cols])

    def middle():
        @pl.loop(0, own)
        def _(e):
            for n in range(ff // 512):
                cols = pl.ds(n * 512, 512)
                h[e, :, cols] = (jax.nn.silu(acc[e, :, cols]) * acc[own + e, :, cols]).astype(BF16)
                acc[e, :, cols] = jnp.zeros((4 * slots, 512), F32)
                acc[own + e, :, cols] = jnp.zeros((4 * slots, 512), F32)

    def to_partner(j):
        return send(pb.at[j % 2], dl.at[j % 2], dls.at[j % 2], dlr.at[j % 2], partner)

    def down(clock):
        s, j = clock // nq, clock % nq
        mine = c == s
        nt = own + 2 * mine.astype(jnp.int32)
        base = j * nt
        held = (j % NT) * 4

        @pl.when(j == 0)
        def _():
            for g in range(3):
                d_start(jnp.int32(g), nt)

        @pl.loop(0, own)
        def _(e):
            d_start(base + e + 3, nt)
            d_wait(base + e)
            v = mm(h[e], dring[(base + e) % 4]).astype(BF16)
            for d in range(4):
                ob[d, e] = v[d * slots : (d + 1) * slots]

        @pl.when(mine)
        def _():
            @pl.loop(0, 4)
            def _(d):
                tot[held + d] = mm(comb[2 * d + s], ob[d].reshape(own * slots, W))

            for t in range(2):
                g = base + own + t
                d_start(g + 3, nt)
                d_wait(g)
                tot[held + z] += mm(sh[t], dring[g % 4])

        @pl.when(jnp.logical_not(mine))
        def _():
            @pl.when(j >= 2)
            def _():
                to_partner(j - 2).wait_send()
                pl.semaphore_wait(free_p, 1)

            @pl.loop(0, 4)
            def _(d):
                pb[j % 2, d] = mm(comb[2 * d + s], ob[d].reshape(own * slots, W)).astype(BF16)

            to_partner(j).start()

    def chain_r(j, d):
        return send(csr.at[j % 2, d - 1], rl.at[j % NL, d - 1], rsend.at[j % 2, d], rrec.at[j % NL, d], right)

    def chain_l(j, d):
        return send(csl.at[j % 2, d], ll.at[j % NL, d], lsend.at[j % 2, d], lrec.at[j % NL, d], left)

    def out_copy(j):
        return pltpu.make_async_copy(yb.at[j % 2], y.at[:, pl.ds(pl.multiple_of(j * W, W), W)], ysem.at[j % 2])

    def collect(clock):
        j = clock - c * nq

        def within(v):
            return (v >= 0) & (v < nq)

        jm = j - 1

        @pl.when(within(jm))
        def _():
            to_partner(jm).wait_recv()

            @pl.loop(0, 4)
            def _(d):
                tot[(jm % NT) * 4 + d] += dl[jm % 2, d].astype(F32)

            @pl.when(jm < nq - 2)
            def _():
                signal(free_p, partner)

        def pass_on(jr, d, first, chain, buf, land, free, to, back):
            @pl.when(jr >= 2)
            def _():
                chain(jr - 2, d).wait_send()

            @pl.when(jr >= NL)
            def _():
                pl.semaphore_wait(free.at[d], 1)

            b = (jr % NT) * 4 + d

            @pl.when(first)
            def _():
                buf[jr % 2] = tot[b].astype(BF16)

            @pl.when(jnp.logical_not(first))
            def _():
                chain(jr, d).wait_recv()
                buf[jr % 2] = (tot[b] + land[jr % NL].astype(F32)).astype(BF16)

                @pl.when(jr < nq - NL)
                def _():
                    signal(free.at[d], back)

            chain(jr, d).start()

        jr = j - 1 - z
        for d in (3, 2, 1):

            @pl.when(within(jr) & (z < d))
            def _():
                pass_on(jr, d, z == 0, chain_r, csr.at[:, d - 1], rl.at[:, d - 1], free_r, right, left)

        jl = j - 1 - (3 - z)
        for d in (0, 1, 2):

            @pl.when(within(jl) & (z > d))
            def _():
                pass_on(jl, d, z == 3, chain_l, csl.at[:, d], ll.at[:, d], free_l, left, right)

        jf = j - 2 - jnp.maximum(z, 3 - z)

        @pl.when(within(jf))
        def _():
            b = (jf % NT) * 4 + z

            @pl.when(z > 0)
            def _():
                chain_r(jf, z).wait_recv()
                tot[b] += rl[jf % NL, z - 1].astype(F32)

                @pl.when(jf < nq - NL)
                def _():
                    signal(free_r.at[z], left)

            @pl.when(z < 3)
            def _():
                chain_l(jf, z).wait_recv()
                tot[b] += ll[jf % NL, z].astype(F32)

                @pl.when(jf < nq - NL)
                def _():
                    signal(free_l.at[z], right)

            @pl.when(jf >= 2)
            def _():
                out_copy(jf - 2).wait()

            yb[jf % 2] = tot[b].astype(BF16)
            out_copy(jf).start()

    @pl.loop(0, 3 * nq + 5)
    def _(u):
        @pl.when(u < 2 * nq)
        def _():
            spread(u + 5)
            up(u)

        @pl.when((u >= nq) & (u < 3 * nq))
        def _():
            down(u - nq)

        @pl.when(u >= nq)
        def _():
            collect(u - nq)

        @pl.when((u == nq - 1) | (u == 2 * nq - 1))
        def _():
            middle()

    for q in (nq - 2, nq - 1):
        for src in range(4):

            @pl.when((z >= src) & (z < 3))
            def _():
                hop(q, src, 0, right).wait_send()

            @pl.when((z <= src) & (z > 0))
            def _():
                hop(q, src, 1, left).wait_send()

            hop(q, src, 2, partner).wait_send()
        for d in range(1, 4):

            @pl.when(z < d)
            def _():
                chain_r(q, d).wait_send()

        for d in range(3):

            @pl.when(z > d)
            def _():
                chain_l(q, d).wait_send()

        to_partner(q).wait_send()
        out_copy(q).wait()


def moe(x, disp, comb, wg, wu, wd, sg, su, sd):
    tokens, depth = x.shape
    own, _, ff = wg.shape
    rows = disp.shape[1]
    slots = rows // own
    nq = depth // W
    dma, regular = pltpu.SemaphoreType.DMA, pltpu.SemaphoreType.REGULAR
    hbm, vmem = pl.BlockSpec(memory_space=pl.ANY), pl.BlockSpec(memory_space=pltpu.VMEM)
    return pl.pallas_call(
        kernel,
        out_shape=jax.ShapeDtypeStruct((tokens, depth), BF16),
        in_specs=[hbm, vmem, vmem] + [hbm] * 6,
        out_specs=hbm,
        scratch_shapes=[
            pltpu.VMEM((2 * nq, 4, tokens, W), BF16),
            pltpu.VMEM((2 * own, 4 * slots, ff), F32),
            pltpu.VMEM((4 * NT, tokens, W), F32),
            pltpu.VMEM((own, 4 * slots, ff), BF16),
            pltpu.VMEM((2, tokens, ff), BF16),
            pltpu.VMEM((4, 2 * W, ff), BF16),
            pltpu.VMEM((4, ff, W), BF16),
            pltpu.VMEM((own, 4, slots, 2 * W), BF16),
            pltpu.VMEM((4, own, slots, W), BF16),
            pltpu.VMEM((2, 4, tokens, W), BF16),
            pltpu.VMEM((2, 4, tokens, W), BF16),
            pltpu.VMEM((NL, 3, tokens, W), BF16),
            pltpu.VMEM((NL, 3, tokens, W), BF16),
            pltpu.VMEM((2, 3, tokens, W), BF16),
            pltpu.VMEM((2, 3, tokens, W), BF16),
            pltpu.VMEM((2, tokens, W), BF16),
            dma((2 * nq, 4)),
            dma((3, 4, 2)),
            dma((4,)),
            dma((4,)),
            dma((2,)),
            dma((2,)),
            dma((NL, 4)),
            dma((NL, 4)),
            dma((2, 4)),
            dma((2, 4)),
            dma((2,)),
            regular((4,)),
            regular((4,)),
            regular,
        ],
        compiler_params=pltpu.CompilerParams(
            collective_id=0, has_side_effects=True, vmem_limit_bytes=67_043_328
        ),
    )(x, disp, comb, wg, wu, wd, sg, su, sd)


def solution(mesh):
    members = mesh.shape["ep"]

    def local(x, expert, slot, gate, w_gate, w_up, w_down, s_gate, s_up, s_down):
        own, (tokens, top) = w_gate.shape[0], expert.shape[2:]
        experts = own * members
        slots = 5 * tokens * top // (4 * experts)
        rows = own * slots
        me = lax.axis_index("ep")
        place = jnp.where(slot[0, 0] < slots, expert[0, 0] * slots + slot[0, 0], -1)
        place = lax.all_gather(place, "ep") - me * rows
        gates = lax.all_gather(gate[0, 0], "ep").astype(BF16)
        hit = place[..., None] == lax.broadcasted_iota(jnp.int32, (1, 1, 1, rows), 3)
        dispatch = jnp.any(hit, axis=2).astype(BF16).transpose(0, 2, 1)
        combine = jnp.sum(jnp.where(hit, gates[..., None].astype(F32), 0.0), axis=2).astype(BF16)
        y = moe(x[0, 0], dispatch, combine, w_gate, w_up, w_down, s_gate, s_up, s_down)
        return y[None, None]

    by_token = P("dp", "ep", None, None)
    by_expert = P("ep", None, None)
    whole = P(None, None)
    return jax.shard_map(
        local,
        mesh=mesh,
        in_specs=(by_token,) * 4 + (by_expert,) * 3 + (whole,) * 3,
        out_specs=by_token,
        check_vma=False,
    )
```

time: 633 us -> 423 us (0.67)
  Pallas kernels: 0 us -> 380 us
  waiting for transfers between devices: 336 us -> 0 us
  matrix products: 220 us -> 0 us
  local copies, waits for them, and re-layouts: 18.3 us -> 4.75 us
  between operations: 13.4 us -> 0.03 us
    pallas_call x0 -> x1, Pallas kernels: none -> 380 us  [moe(): pl.pallas_call(kernel, out_shape=jax.ShapeDtypeStruct((tokens, depth), BF...]
    dot_general x7 -> x0, matrix products: 220 us -> none  [dot(): return jnp.einsum(form, a, b, preferred_element_type=F32)]
    reduce_scatter x1 -> x0, waiting for transfers between devices: 186 us -> none  [local(): y = lax.psum_scatter(y, 'ep', scatter_dimension=0, tiled=False)]
    all_gather x1 -> x0, waiting for transfers between devices: 149 us -> none  [local(): everyone = lax.all_gather(x, 'ep')]
    convert_element_type x1, local copies, waits for them, and re-layouts: 16.5 us -> 1.31 us  [local(): jnp.sum(jnp.where(hit, gates[..., None].astype(F32), 0.0), axis=2)]
  transfers between devices with their start and end apart: 2 -> 0, of which waited for: 2 -> 0; matrix products, arithmetic and copies ran while one was open for 4% -> 0% of each run, Pallas kernels for 0% -> 0%
where the time goes in v2:
time: 423 us; the launch traced here: 422 us
  Pallas kernels  380 us (90%)
  blocking collectives  29.4 us (7%)
  other arithmetic  7.82 us (2%)
  local copies, waits for them, and re-layouts  4.75 us (1%)
    pallas_call x1, Pallas kernels, moe(): pl.pallas_call(kernel, out_shape=jax.ShapeDtypeStruct((tokens, depth), BF...  380 us
    all_gather x1, blocking collectives, local(): gates = lax.all_gather(gate[0, 0], 'ep').astype(BF16)  15.4 us
    all_gather x1, blocking collectives, local(): place = lax.all_gather(place, 'ep') - me * rows  13.9 us

profile of v2, /device:TPU:1, one launch (start us, length us, event | category | flops | bytes accessed | tf_op | source)
XLA Modules:
  0.0 422.3 jit_solution(9369852142834400214)
XLA Ops:
  0.0 0.7 compare_select_fusion
  0.7 0.7 convert.3
  1.4 15.4 %all-gather.1 = bf16[8,1,256,6]{2,1,3,0:T(2,128)(2,1)S(1)} all-gather(bf16[1,1,256,6]{2,1,3,0:T(2,128)(2,1)S(1)} %convert.3), channel_id=3, replica_groups=mesh['dp'=4,'ep'=8] {'ep'}, dimensions={0}, use_global_device_ids=true | all-gather | bytes 27648 | tf_op jit(solution)/shard_map/all_gather | solution.py:488
  16.9 13.9 %all-gather = s32[8,1,256,6]{2,1,3,0:T(1,128)S(1)} all-gather(s32[1,1,256,6]{2,1,3,0:T(1,128)S(1)} %compare_select_fusion), channel_id=2, replica_groups=mesh['dp'=4,'ep'=8] {'ep'}, dimensions={0}, use_global_device_ids=true | all-gather | bytes 55296 | tf_op jit(solution)/shard_map/all_gather | solution.py:487
  30.8 3.2 fusion
  34.0 1.2 convert_bitcast_fusion.disp
  35.2 2.0 select_reduce_fusion
  37.2 1.3 copy.34.comb
  38.6 380.4 %shard_map.100 = bf16[256,5120]{1,0:T(8,128)(2,1)} custom-call(bf16[256,5120]{1,0:T(8,128)(2,1)} %bitcast.12, bf16[8,240,256]{2,1,0:T(8,128)(2,1)} %convert_bitcast_fusion.disp, bf16[8,256,240]{2,1,0:T(8,128)(2,1)} %copy.34.comb, bf16[5,5120,1536]{2,1,0:T(8,128)(2,1)} %wg.1, bf16[5,5120,1536]{2,1,0:T(8,128)(2,1)} %wu.1, bf16[5,1536,5120]{2,1,0:T(8,128)(2,1)} %wd.1, ...), custom_call_target="tpu_custom_call" | custom-call | tf_op jit(solution)/shard_map/pallas_call | solution.py:434
  418.9 3.4 copy.44
  (4 shorter events, 0.0 us)

commit v3 on v2

--- a/solution.py
+++ b/solution.py
@@ -10,7 +10,7 @@
 F32 = jnp.float32
 BF16 = jnp.bfloat16
 W = 256
-NL = 6
+NL = 4
 NT = 6
 MESH = pl.DeviceIdType.MESH
 
@@ -20,13 +20,13 @@
 
 
 def kernel(
-    x, disp, comb, wg, wu, wd, sg, su, sd, y,
-    xg, acc, tot, h, sh, gring, dring, zb, ob, pb, dl, rl, ll, csr, csl, yb,
-    agr, ags, gsem, dsem, dlr, dls, rrec, lrec, rsend, lsend, ysem, free_r, free_l, free_p,
+    top, slots,
+    x, place, gate, wg, wu, wd, sg, su, sd, y,
+    places, gates, disp, comb, xg, acc, tot, h, sh, gring, dring, sring, zb, ob, pb, dl, rl, ll, csr, csl, yb,
+    pr, ps, gr, gs, agr, ags, gsem, dsem, ssem, dlr, dls, rrec, lrec, rsend, lsend, ysem, free_r, free_l, free_p,
 ):
     tokens, depth = x.shape
     own, _, ff = wg.shape
-    slots = disp.shape[1] // own
     nq = depth // W
     deep = 2 * W
     me = lax.axis_index("ep")
@@ -41,64 +41,30 @@
     def signal(sem, to):
         pl.semaphore_signal(sem, inc=1, device_id=to, device_id_type=MESH)
 
-    shared_tiles = 4 * (depth // deep)
-    per_pass = 2 * own * (depth // deep)
-    all_tiles = shared_tiles + 2 * per_pass
-
-    def g_copy(src, slot):
-        return pltpu.make_async_copy(src, gring.at[slot], gsem.at[slot])
-
-    def g_start(g):
-        slot = g % 4
-
-        @pl.when(g < shared_tiles)
-        def _():
-            rows = pl.ds((g // 4) * deep, deep)
-            t = g % 4
-
-            @pl.when(t < 2)
-            def _():
-                g_copy(sg.at[rows, pl.ds(pl.multiple_of((t % 2) * ff, 128), ff)], slot).start()
-
-            @pl.when(t >= 2)
-            def _():
-                g_copy(su.at[rows, pl.ds(pl.multiple_of((t % 2) * ff, 128), ff)], slot).start()
-
-        @pl.when((g >= shared_tiles) & (g < all_tiles))
-        def _():
-            r = (g - shared_tiles) % per_pass
-            rows = pl.ds((r // (2 * own)) * deep, deep)
-            t = r % (2 * own)
-
-            @pl.when(t < own)
-            def _():
-                g_copy(wg.at[t % own, rows, :], slot).start()
-
-            @pl.when(t >= own)
-            def _():
-                g_copy(wu.at[t % own, rows, :], slot).start()
+    ahead = 3
+    nk = depth // deep
+    routed_base = 4 * nk
+
+    def g_copy(src, g):
+        return pltpu.make_async_copy(src, gring.at[g % 4], gsem.at[g % 4])
+
+    def shared_tile(t, k):
+        return (sg, su)[t // 2].at[pl.ds(k * deep, deep), pl.ds((t % 2) * ff, ff)]
+
+    def routed_tile(t, k):
+        return (wg, wu)[t % 2].at[t // 2, pl.ds(k * deep, deep), :]
 
     def g_wait(g):
-        g_copy(wg.at[0, pl.ds(0, deep), :], g % 4).wait()
-
-    def d_copy(src, slot):
-        return pltpu.make_async_copy(src, dring.at[slot], dsem.at[slot])
-
-    def d_start(g, nt):
-        slot = g % 4
-        t = g % nt
-        cols = pl.ds(pl.multiple_of((g // nt) * W, W), W)
-
-        @pl.when((g < nq * nt) & (t < own))
-        def _():
-            d_copy(wd.at[t % own, :, cols], slot).start()
-
-        @pl.when((g < nq * nt) & (t >= own))
-        def _():
-            d_copy(sd.at[pl.ds(((t - own) % 2) * ff, ff), cols], slot).start()
-
-    def d_wait(g):
-        d_copy(wd.at[0, :, pl.ds(0, W)], g % 4).wait()
+        g_copy(wg.at[0, pl.ds(0, deep), :], g).wait()
+
+    def piece_cols(j):
+        return pl.ds(pl.multiple_of(j * W, W), W)
+
+    def d_copy(e, j, g):
+        return pltpu.make_async_copy(wd.at[e, :, piece_cols(j)], dring.at[g % 4], dsem.at[g % 4])
+
+    def s_copy(t, j):
+        return pltpu.make_async_copy(sd.at[pl.ds(t * ff, ff), piece_cols(j)], sring.at[t], ssem.at[t])
 
     def hop(q, src, kind, to):
         piece = xg.at[c * nq + q, src]
@@ -111,49 +77,64 @@
 
         hop(q, src, kind, to).start()
 
+    def leave(q):
+        @pl.when((q >= 0) & (q < nq))
+        def _():
+            @pl.when(z < 3)
+            def _():
+                hop_start(q, z, 0, right)
+
+            @pl.when(z > 0)
+            def _():
+                hop_start(q, z, 1, left)
+
+            hop_start(q, z, 2, partner)
+
     def spread(clock):
-        for src in range(4):
+        for src in (0, 3, 1, 2):
             q = clock - c * nq - jnp.abs(z - src)
 
-            @pl.when((q >= 0) & (q < nq))
-            def _():
-                @pl.when(z != src)
-                def _():
-                    hop(q, src, 0, right).wait_recv()
-
-                @pl.when((z >= src) & (z < 3))
+            @pl.when((q >= 0) & (q < nq) & (z != src))
+            def _():
+                hop(q, src, 0, right).wait_recv()
+
+                @pl.when((z > src) & (z < 3))
                 def _():
                     hop_start(q, src, 0, right)
 
-                @pl.when((z <= src) & (z > 0))
+                @pl.when((z < src) & (z > 0))
                 def _():
                     hop_start(q, src, 1, left)
 
                 hop_start(q, src, 2, partner)
+
+        leave(clock - c * nq + 1)
 
     def own_piece(q):
         return pltpu.make_async_copy(
             x.at[:, pl.ds(pl.multiple_of(q * W, W), W)], xg.at[c * nq + q, z], agr.at[c * nq + q, z]
         )
 
+    others = 2 * 4 - 1
+
+    def place_to(o, src, to):
+        return send(place, places.at[src], ps.at[o], pr.at[src], to)
+
+    def gate_to(o, src, to):
+        return send(gate, gates.at[src], gs.at[o], gr.at[src], to)
+
     barrier = pltpu.get_barrier_semaphore()
-
-    @pl.when(z > 0)
-    def _():
-        signal(barrier, left)
-
-    @pl.when(z < 3)
-    def _():
-        signal(barrier, right)
-
-    signal(barrier, partner)
+    for o in range(others):
+        signal(barrier, {"ep": (me + o + 1) % (others + 1)})
 
     @pl.loop(0, nq)
     def _(q):
         own_piece(q).start()
 
-    for g in range(3):
-        g_start(jnp.int32(g))
+    for g in range(ahead):
+        g_copy(shared_tile(g, 0), g).start()
+    for t in range(2):
+        s_copy(t, 0).start()
 
     @pl.loop(0, 4 * NT)
     def _(b):
@@ -167,23 +148,62 @@
     def _(q):
         own_piece(q).wait()
 
-    pl.semaphore_wait(barrier, 1 + (z > 0).astype(jnp.int32) + (z < 3).astype(jnp.int32))
-
-    @pl.loop(0, depth // deep)
-    def _(k):
-        @pl.when(k % 2 == 0)
-        def _():
-            spread(k // 2)
-
-        @pl.loop(0, 4)
-        def _(t):
-            g = 4 * k + t
-            g_start(g + 3)
+    pl.semaphore_wait(barrier, others)
+    leave(-c * nq)
+    for o in range(others):
+        to = {"ep": (me + o + 1) % (others + 1)}
+        place_to(o, me, to).start()
+        gate_to(o, me, to).start()
+    places[me] = place[...]
+    gates[me] = gate[...]
+
+    def first_half(k, last):
+        a = [xg[c * nq + 2 * k + i, z] for i in range(2)]
+        for t in range(4):
+            g, later = 4 * k + t, t + ahead
+            if later < 4:
+                tile = shared_tile(later, k)
+            else:
+                tile = routed_tile(later - 4, 0) if last else shared_tile(later - 4, k + 1)
+            g_copy(tile, g + ahead).start()
             g_wait(g)
-            a = [xg[c * nq + 2 * k + i, z] for i in range(2)]
             for n in range(ff // W):
                 w = gring.at[g % 4, :, pl.ds(n * W, W)]
                 tot[t * (ff // W) + n] += mm(a[0], w[:W]) + mm(a[1], w[W:])
+
+    @pl.loop(0, nk - 1)
+    def _(k):
+        @pl.when(k % 3 != 2)
+        def _():
+            spread(k // 3 * 2 + k % 3)
+
+        first_half(k, False)
+
+    early = (nk - 1) // 3 * 2
+    spread(jnp.int32(early))
+    first_half(nk - 1, True)
+
+    for o in range(others):
+        src = (me + o + 1) % (others + 1)
+        place_to(o, src, partner).wait()
+        gate_to(o, src, partner).wait()
+
+    rows = own * slots
+
+    @pl.loop(0, others + 1)
+    def _(src):
+        at = places[src] - me * rows
+        at = jnp.where((at >= 0) & (at < rows), at, -1)
+        weight = gates[src]
+        row = lax.broadcasted_iota(jnp.int32, (tokens, tokens), 0)
+        one = jnp.zeros((tokens, tokens), F32)
+        weighted = jnp.zeros((tokens, tokens), F32)
+        for k in range(top):
+            hit = row == at[k : k + 1]
+            one = jnp.where(hit, 1.0, one)
+            weighted = jnp.where(hit, weight[k : k + 1], weighted)
+        disp[src] = one[:rows].astype(BF16)
+        comb[src] = weighted.T[:, :rows].astype(BF16)
 
     half = 2 * ff // W
     for n in range(half):
@@ -202,22 +222,26 @@
                         piece = xg.at[s * nq + 2 * k + i, src]
                         send(piece, piece, ags.at[0, src, 0], agr.at[s * nq + 2 * k + i, src], partner).wait_recv()
 
-            @pl.loop(0, 4)
-            def _(src):
-                for i in range(2):
-                    v = mm(disp[2 * src + s], xg[s * nq + 2 * k + i, src]).astype(BF16)
-                    for e in range(own):
-                        zb[e, src, :, pl.ds(i * W, W)] = v[e * slots : (e + 1) * slots]
-
-        @pl.loop(0, own)
-        def _(e):
-            g = shared_tiles + u * own + e
-            g_start(g + 3)
-            g_wait(g)
-            a = zb[e].reshape(4 * slots, deep)
-            for n in range(ff // 512):
-                cols = pl.ds(n * 512, 512)
-                acc[part * own + e, :, cols] += mm(a, gring[g % 4, :, cols])
+        for half in range(2):
+
+            @pl.when(part == half)
+            def _():
+                if half == 0:
+                    for src in range(4):
+                        for i in range(2):
+                            v = mm(disp[2 * src + s], xg[s * nq + 2 * k + i, src]).astype(BF16)
+                            for e in range(own):
+                                zb[e, src, :, pl.ds(i * W, W)] = v[e * slots : (e + 1) * slots]
+                for i in range(own):
+                    t, g = half * own + i, routed_base + u * own + i
+                    later = t + ahead
+                    tile = routed_tile(later % (2 * own), k if later < 2 * own else (k + 1) % nk)
+                    g_copy(tile, g + ahead).start()
+                    g_wait(g)
+                    a = zb[t // 2].reshape(4 * slots, deep)
+                    for n in range(ff // 512):
+                        cols = pl.ds(n * 512, 512)
+                        acc[t % 2 * own + t // 2, :, cols] += mm(a, gring[g % 4, :, cols])
 
     def middle():
         @pl.loop(0, own)
@@ -234,34 +258,39 @@
     def down(clock):
         s, j = clock // nq, clock % nq
         mine = c == s
-        nt = own + 2 * mine.astype(jnp.int32)
-        base = j * nt
+        base = j * own
         held = (j % NT) * 4
 
         @pl.when(j == 0)
         def _():
-            for g in range(3):
-                d_start(jnp.int32(g), nt)
-
-        @pl.loop(0, own)
-        def _(e):
-            d_start(base + e + 3, nt)
-            d_wait(base + e)
+            for g in range(ahead):
+                d_copy(g, 0, g).start()
+
+        for e in range(own):
+            later = e + ahead
+            d_copy(later % own, j if later < own else jnp.minimum(j + 1, nq - 1), base + later).start()
+            d_copy(0, 0, base + e).wait()
             v = mm(h[e], dring[(base + e) % 4]).astype(BF16)
             for d in range(4):
                 ob[d, e] = v[d * slots : (d + 1) * slots]
 
+        @pl.when(j == nq - 1)
+        def _():
+            for i in range(ahead):
+                d_copy(0, 0, base + own + i).wait()
+
         @pl.when(mine)
         def _():
-            @pl.loop(0, 4)
-            def _(d):
+            for d in range(4):
                 tot[held + d] = mm(comb[2 * d + s], ob[d].reshape(own * slots, W))
-
             for t in range(2):
-                g = base + own + t
-                d_start(g + 3, nt)
-                d_wait(g)
-                tot[held + z] += mm(sh[t], dring[g % 4])
+                s_copy(t, 0).wait()
+            tot[held + z] += mm(sh[0], sring[0]) + mm(sh[1], sring[1])
+
+            @pl.when(j < nq - 1)
+            def _():
+                for t in range(2):
+                    s_copy(t, j + 1).start()
 
         @pl.when(jnp.logical_not(mine))
         def _():
@@ -270,10 +299,8 @@
                 to_partner(j - 2).wait_send()
                 pl.semaphore_wait(free_p, 1)
 
-            @pl.loop(0, 4)
-            def _(d):
+            for d in range(4):
                 pb[j % 2, d] = mm(comb[2 * d + s], ob[d].reshape(own * slots, W)).astype(BF16)
-
             to_partner(j).start()
 
     def chain_r(j, d):
@@ -380,7 +407,7 @@
     def _(u):
         @pl.when(u < 2 * nq)
         def _():
-            spread(u + 5)
+            spread(u + early + 1)
             up(u)
 
         @pl.when((u >= nq) & (u < 3 * nq))
@@ -395,6 +422,8 @@
         def _():
             middle()
 
+    for i in range(ahead):
+        g_wait(routed_base + 2 * nq * own + i)
     for q in (nq - 2, nq - 1):
         for src in range(4):
 
@@ -423,20 +452,24 @@
         out_copy(q).wait()
 
 
-def moe(x, disp, comb, wg, wu, wd, sg, su, sd):
+def moe(x, place, gate, top, slots, wg, wu, wd, sg, su, sd):
     tokens, depth = x.shape
     own, _, ff = wg.shape
-    rows = disp.shape[1]
-    slots = rows // own
+    rows = own * slots
+    padded = place.shape[0]
     nq = depth // W
     dma, regular = pltpu.SemaphoreType.DMA, pltpu.SemaphoreType.REGULAR
     hbm, vmem = pl.BlockSpec(memory_space=pl.ANY), pl.BlockSpec(memory_space=pltpu.VMEM)
     return pl.pallas_call(
-        kernel,
+        functools.partial(kernel, top, slots),
         out_shape=jax.ShapeDtypeStruct((tokens, depth), BF16),
         in_specs=[hbm, vmem, vmem] + [hbm] * 6,
         out_specs=hbm,
         scratch_shapes=[
+            pltpu.VMEM((8, padded, tokens), jnp.int32),
+            pltpu.VMEM((8, padded, tokens), F32),
+            pltpu.VMEM((8, rows, tokens), BF16),
+            pltpu.VMEM((8, tokens, rows), BF16),
             pltpu.VMEM((2 * nq, 4, tokens, W), BF16),
             pltpu.VMEM((2 * own, 4 * slots, ff), F32),
             pltpu.VMEM((4 * NT, tokens, W), F32),
@@ -444,6 +477,7 @@
             pltpu.VMEM((2, tokens, ff), BF16),
             pltpu.VMEM((4, 2 * W, ff), BF16),
             pltpu.VMEM((4, ff, W), BF16),
+            pltpu.VMEM((2, ff, W), BF16),
             pltpu.VMEM((own, 4, slots, 2 * W), BF16),
             pltpu.VMEM((4, own, slots, W), BF16),
             pltpu.VMEM((2, 4, tokens, W), BF16),
@@ -453,10 +487,15 @@
             pltpu.VMEM((2, 3, tokens, W), BF16),
             pltpu.VMEM((2, 3, tokens, W), BF16),
             pltpu.VMEM((2, tokens, W), BF16),
+            dma((8,)),
+            dma((7,)),
+            dma((8,)),
+            dma((7,)),
             dma((2 * nq, 4)),
             dma((3, 4, 2)),
             dma((4,)),
             dma((4,)),
+            dma((2,)),
             dma((2,)),
             dma((2,)),
             dma((NL, 4)),
@@ -471,7 +510,7 @@
         compiler_params=pltpu.CompilerParams(
             collective_id=0, has_side_effects=True, vmem_limit_bytes=67_043_328
         ),
-    )(x, disp, comb, wg, wu, wd, sg, su, sd)
+    )(x, place, gate, wg, wu, wd, sg, su, sd)
 
 
 def solution(mesh):
@@ -481,15 +520,11 @@
         own, (tokens, top) = w_gate.shape[0], expert.shape[2:]
         experts = own * members
         slots = 5 * tokens * top // (4 * experts)
-        rows = own * slots
-        me = lax.axis_index("ep")
-        place = jnp.where(slot[0, 0] < slots, expert[0, 0] * slots + slot[0, 0], -1)
-        place = lax.all_gather(place, "ep") - me * rows
-        gates = lax.all_gather(gate[0, 0], "ep").astype(BF16)
-        hit = place[..., None] == lax.broadcasted_iota(jnp.int32, (1, 1, 1, rows), 3)
-        dispatch = jnp.any(hit, axis=2).astype(BF16).transpose(0, 2, 1)
-        combine = jnp.sum(jnp.where(hit, gates[..., None].astype(F32), 0.0), axis=2).astype(BF16)
-        y = moe(x[0, 0], dispatch, combine, w_gate, w_up, w_down, s_gate, s_up, s_down)
+        place = jnp.where(slot[0, 0] < slots, expert[0, 0] * slots + slot[0, 0], -1).T
+        weight = gate[0, 0].astype(BF16).astype(F32).T
+        pad = ((0, -top % 8), (0, 0))
+        place, weight = jnp.pad(place, pad, constant_values=-1), jnp.pad(weight, pad)
+        y = moe(x[0, 0], place, weight, top, slots, w_gate, w_up, w_down, s_gate, s_up, s_down)
         return y[None, None]
 
     by_token = P("dp", "ep", None, None)

time: 423 us -> 376 us (0.89)
  blocking collectives: 29.4 us -> 0 us
  Pallas kernels: 380 us -> 369 us
  other arithmetic: 7.82 us -> 1.31 us
    all_gather x2 -> x0, blocking collectives: 29.4 us -> none  [the longest x1 15.4 us: local(): gates = lax.all_gather(gate[0, 0], 'ep').astype(BF16)]
    pallas_call x1, Pallas kernels: 380 us -> 369 us  [moe(): pl.pallas_call(functools.partial(kernel, top, slots), out_shape=jax.Shape...]
where the time goes in v3:
time: 376 us; the launch traced here: 375 us
  Pallas kernels  369 us (98%)
  local copies, waits for them, and re-layouts  4.7 us (1%)
    pallas_call x1, Pallas kernels, moe(): pl.pallas_call(functools.partial(kernel, top, slots), out_shape=jax.Shape...  369 us

profile of v3, /device:TPU:1, one launch (start us, length us, event | category | flops | bytes accessed | tf_op | source)
XLA Modules:
  0.0 375.1 jit_solution(5387069546546138705)
XLA Ops:
  0.0 0.7 copy.29
  0.7 0.6 pad_convert_fusion.gate
  1.3 0.7 fusion.1
  2.0 0.6 pad.10.place
  2.6 369.1 %shard_map.100 = bf16[256,5120]{1,0:T(8,128)(2,1)} custom-call(bf16[256,5120]{1,0:T(8,128)(2,1)} %bitcast.12, s32[8,256]{1,0:T(8,128)} %pad.10.place, f32[8,256]{1,0:T(8,128)} %pad_convert_fusion.gate, bf16[5,5120,1536]{2,1,0:T(8,128)(2,1)} %wg.1, bf16[5,5120,1536]{2,1,0:T(8,128)(2,1)} %wu.1, bf16[5,1536,5120]{2,1,0:T(8,128)(2,1)} %wd.1, ...), custom_call_target="tpu_custom_call" | custom-call | tf_op jit(solution)/shard_map/pallas_call | solution.py:463
  371.7 3.4 copy.31

commit v4 on v3

--- a/solution.py
+++ b/solution.py
@@ -173,15 +173,15 @@
 
     @pl.loop(0, nk - 1)
     def _(k):
-        @pl.when(k % 3 != 2)
-        def _():
-            spread(k // 3 * 2 + k % 3)
+        @pl.when(k % 2 == 0)
+        def _():
+            spread(k // 2)
 
         first_half(k, False)
 
-    early = (nk - 1) // 3 * 2
+    first_half(nk - 1, True)
+    early = nk // 2
     spread(jnp.int32(early))
-    first_half(nk - 1, True)
 
     for o in range(others):
         src = (me + o + 1) % (others + 1)
@@ -407,7 +407,10 @@
     def _(u):
         @pl.when(u < 2 * nq)
         def _():
-            spread(u + early + 1)
+            @pl.when(u > 0)
+            def _():
+                spread(u + early)
+
             up(u)
 
         @pl.when((u >= nq) & (u < 3 * nq))

time: 376 us -> 364 us (0.968)
  Pallas kernels: 369 us -> 358 us
    pallas_call x1, Pallas kernels: 369 us -> 358 us  [moe(): pl.pallas_call(functools.partial(kernel, top, slots), out_shape=jax.Shape...]
where the time goes in v4:
time: 364 us
  Pallas kernels  358 us (98%)
  local copies, waits for them, and re-layouts  4.7 us (1%)
    pallas_call x1, Pallas kernels, moe(): pl.pallas_call(functools.partial(kernel, top, slots), out_shape=jax.Shape...  358 us

profile of v4, /device:TPU:1, one launch (start us, length us, event | category | flops | bytes accessed | tf_op | source)
XLA Modules:
  0.0 364.0 jit_solution(14519583696176143148)
XLA Ops:
  0.0 0.7 copy.29
  0.7 0.6 pad_convert_fusion.gate
  1.3 0.7 fusion.1
  2.0 0.6 pad.10.place
  2.6 358.0 %shard_map.100 = bf16[256,5120]{1,0:T(8,128)(2,1)} custom-call(bf16[256,5120]{1,0:T(8,128)(2,1)} %bitcast.12, s32[8,256]{1,0:T(8,128)} %pad.10.place, f32[8,256]{1,0:T(8,128)} %pad_convert_fusion.gate, bf16[5,5120,1536]{2,1,0:T(8,128)(2,1)} %wg.1, bf16[5,5120,1536]{2,1,0:T(8,128)(2,1)} %wu.1, bf16[5,1536,5120]{2,1,0:T(8,128)(2,1)} %wd.1, ...), custom_call_target="tpu_custom_call" | custom-call | tf_op jit(solution)/shard_map/pallas_call | solution.py:466
  360.6 3.4 copy.31
